TPU v7x, 32 devices: a whole 2x2x4 slice. The times are simulated.
32 devices in a mesh: rep: 4 (over z), row: 4 (over x, core), col: 2 (over y).
Axes of the slice: x: 2, y: 2, z: 4, core: 2. Of those that a mesh axis runs over, the one named last changes fastest.
Arguments:
- grad_parts: bfloat16 [4, 16384, 6144], P('rep', ('row', 'col')), may hold values from -0.03125 to 0.03125, as said below
- statistic: float32 [6144, 6144], P('row', 'col'), may hold values from -150 to 150, as said below
Outputs:
- gram_matrix: float32 [6144, 6144], P('row', 'col')
- statistic_next: float32 [6144, 6144], P('row', 'col')
Inputs may be any that keep to these rules, and one draw needn't show every extreme that they name: Every entry of grad_parts has a magnitude between 2^-10 and 2^-5. statistic is symmetric and positive definite.
All inputs are finite; a program needn't handle non-finite values.
Results may differ from a plain program's by a relative error of at most 0.008.
Values may be sent and summed in bfloat16 or wider, within the bound.
A program may use at most 192 MiB of HBM per device.

v0:
```python
import jax
import jax.numpy as jnp
from jax import lax
from jax.sharding import PartitionSpec as P


def shards(grad_parts, statistic):
    own_part = grad_parts[0].astype(jnp.float32)
    summed = lax.psum_scatter(own_part.astype(jnp.bfloat16), "rep", scatter_dimension=0, tiled=True)
    rows_panel = lax.all_to_all(summed, "row", split_axis=1, concat_axis=0, tiled=True)
    cols_panel = lax.all_to_all(summed, "col", split_axis=1, concat_axis=0, tiled=True)
    row_count = lax.axis_size("row")
    col_count = lax.axis_size("col")
    quarter = summed.shape[0]
    left_whole = lax.all_gather(rows_panel, "col", axis=0, tiled=True)
    left_order = (
        left_whole.reshape(col_count, row_count, quarter, -1)
        .transpose(1, 0, 2, 3)
        .reshape(row_count * col_count * quarter, -1)
    )
    partial_tile = lax.dot_general(
        left_order,
        lax.all_gather(cols_panel, "row", axis=0, tiled=True),
        (((0,), (0,)), ((), ())),
        preferred_element_type=jnp.float32,
    )
    gram_tile = lax.psum(partial_tile, "rep")
    return (gram_tile, 0.95 * statistic + 0.05 * gram_tile)


def solution(mesh):
    return jax.shard_map(
        shards,
        mesh=mesh,
        in_specs=(P("rep", ("row", "col"), None), P("row", "col")),
        out_specs=(P("row", "col"), P("row", "col")),
        check_vma=False,
    )
```

profile of v0, /device:TPU:0, one launch (start us, length us, event | category | flops | bytes accessed | tf_op | source)
XLA Modules:
  0.0 1626.5 jit_solution(12246390620208611394)
XLA Ops:
  7.2 0.0 reduce-scatter.2.cloned.1.call-start
  7.2 30.3 %copy.5 = bf16[1,2048,6144]{1,2,0:T(8,128)(2,1)} copy(bf16[1,2048,6144]{2,1,0:T(8,128)(2,1)} %param.2) | data formatting | bytes 50331648 | tf_op args[0]
  37.5 0.0 reduce-scatter.2.cloned.1.call-update
  37.6 0.0 all-gather.3.cloned.1.call-start
  37.6 417.0 %reduce-scatter.2.cloned.1.call-done = bf16[512,6144]{0,1:T(8,128)(2,1)} async-done(((bf16[2048,6144]{0,1:T(8,128)(2,1)}), bf16[512,6144]{0,1:T(8,128)(2,1)}) %reduce-scatter.2.cloned.1.call-update) | async-done | bytes 6291472 | tf_op jit(solution)/shard_map/reduce_scatter | solution.py:9
  454.7 77.3 %all_to_all.38 = bf16[512,4,1536]{0,2,1:T(8,128)(2,1)} all-to-all(bf16[512,4,1536]{0,2,1:T(8,128)(2,1)} %bitcast.15), channel_id=1, replica_groups=mesh['rep'=4,'row'=4,'col'=2] {'row'}, dimensions={1} | all-to-all | bytes 12582912 | tf_op jit(solution)/shard_map/all_to_all | solution.py:10
  532.0 8.6 copy.6
  540.6 0.0 all-gather.3.cloned.1.call-update
  540.6 0.0 all-gather.5.cloned.1.call-start
  540.7 140.8 %all_to_all.39 = bf16[512,2,3072]{0,2,1:T(8,128)(2,1)} all-to-all(bf16[512,2,3072]{0,2,1:T(8,128)(2,1)} %bitcast.16), channel_id=1, replica_groups=mesh['rep'=4,'row'=4,'col'=2] {'col'}, dimensions={1} | all-to-all | bytes 12582912 | tf_op jit(solution)/shard_map/all_to_all | solution.py:11
  681.4 8.6 copy.8
  690.1 0.0 all-gather.5.cloned.1.call-update
  690.1 0.0 all-reduce.2.cloned.1.call-start
  690.2 64.5 %all-gather.3.cloned.1.call-done = bf16[4096,1536]{1,0:T(8,128)(2,1)} async-done(((bf16[2048,1536]{1,0:T(8,128)(2,1)}), bf16[4096,1536]{1,0:T(8,128)(2,1)}) %all-gather.3.cloned.1.call-update) | async-done | bytes 12582928 | tf_op jit(solution)/shard_map/all_gather | solution.py:15
  754.7 11.1 copy.7
  765.8 145.7 %all-gather.5.cloned.1.call-done = bf16[4096,3072]{1,0:T(8,128)(2,1)} async-done(((bf16[1024,3072]{1,0:T(8,128)(2,1)}), bf16[4096,3072]{1,0:T(8,128)(2,1)}) %all-gather.5.cloned.1.call-update) | async-done | bytes 25165840 | tf_op jit(solution)/shard_map/all_gather | solution.py:23
  911.5 48.0 %fusion = f32[1536,3072]{1,0:T(8,128)} fusion(bf16[4096,1536]{1,0:T(8,128)(2,1)} %bitcast.21, bf16[4096,3072]{1,0:T(8,128)(2,1)} %all-gather.5.cloned.1.call-done), kind=kOutput, calls=%fused_computation.1 | convolution fusion | flops 38654705664 | bytes 56623104 | tf_op jit(solution)/shard_map/dot_general | solution.py:21
  959.5 0.0 all-reduce.2.cloned.1.call-update
  959.6 629.5 %all-reduce.2.cloned.1.call-done = f32[1536,3072]{1,0:T(8,128)} async-done(((f32[1536,3072]{1,0:T(8,128)}), f32[1536,3072]{1,0:T(8,128)}) %all-reduce.2.cloned.1.call-update) | async-done | bytes 18874384 | tf_op jit(solution)/shard_map/psum | solution.py:27
  1589.1 0.0 copy-start
  1589.1 20.7 %multiply_add_fusion = f32[1536,3072]{1,0:T(8,128)} fusion(f32[1536,3072]{1,0:T(8,128)} %all-reduce.2.cloned.1.call-done, f32[1536,3072]{1,0:T(8,128)} %param.3), kind=kLoop, calls=%fused_computation | loop fusion | flops 14155776 | bytes 56623104 | tf_op jit(solution)/shard_map/add | solution.py:28
  1609.8 3.3 copy-done
  1613.1 6.8 copy.10
Async XLA Ops:
  7.2 447.5 %reduce-scatter.2.cloned.1.call-start = ((), (), s32[]{:S(2)}) async-start(), calls=%async_computation.3 | async-start | bytes 31457280 | tf_op jit(solution)/shard_map/reduce_scatter | solution.py:9
  37.6 717.1 %all-gather.3.cloned.1.call-start = ((), (), s32[]{:S(2)}) async-start(), calls=%async_computation.4 | async-start | bytes 18874368 | tf_op jit(solution)/shard_map/all_gather | solution.py:15
  540.6 370.9 %all-gather.5.cloned.1.call-start = ((), (), s32[]{:S(2)}) async-start(), calls=%async_computation.5 | async-start | bytes 31457280 | tf_op jit(solution)/shard_map/all_gather | solution.py:23
  690.1 899.0 %all-reduce.2.cloned.1.call-start = ((), (), s32[]{:S(2)}) async-start(), calls=%async_computation.6 | async-start | bytes 37748736 | tf_op jit(solution)/shard_map/psum | solution.py:27
  1589.1 24.0 %copy-start = (f32[1536,3072]{1,0:T(8,128)S(1)}, f32[1536,3072]{1,0:T(8,128)}, u32[]{:S(2)}) copy-start(f32[1536,3072]{1,0:T(8,128)} %all-reduce.2.cloned.1.call-done) | copy-start | bytes 56623108
Sparse Core Ops, SparseCore 0:
  37.7 416.9 reduce-scatter.1
  540.7 213.8 all-gather.2
  756.2 155.2 all-gather.4
  959.7 629.3 all-reduce.1
where the time goes:
time: 1630 us
  waiting for transfers between devices  1260 us (77%)
  blocking collectives  218 us (13%)
  local copies, waits for them, and re-layouts  68.9 us (4%)
  matrix products  48 us (3%)
  other arithmetic  20.7 us (1%)
    psum x1, waiting for transfers between devices, shards(): gram_tile = lax.psum(partial_tile, 'rep')  630 us
    reduce_scatter x1, waiting for transfers between devices, shards(): lax.psum_scatter(own_part.astype(jnp.bfloat16), 'rep', scatter_dimension=...  417 us
    all_gather x1, waiting for transfers between devices, shards(): lax.all_gather(cols_panel, 'row', axis=0, tiled=True)  146 us
    all_to_all x1, blocking collectives, shards(): lax.all_to_all(summed, 'col', split_axis=1, concat_axis=0, tiled=True)  141 us
    all_to_all x1, blocking collectives, shards(): lax.all_to_all(summed, 'row', split_axis=1, concat_axis=0, tiled=True)  77.3 us
    all_gather x1, waiting for transfers between devices, shards(): left_whole = lax.all_gather(rows_panel, 'col', axis=0, tiled=True)  64.5 us
    dot_general x1, matrix products, shards(): lax.dot_general(left_order, lax.all_gather(cols_panel, 'row', axis=0, til...  48 us
    unnamed x4, local copies, waits for them, and re-layouts  40.5 us
  transfers between devices with their start and end apart: 4, of which 4 were waited for; matrix products, arithmetic and copies ran while one was open for 1% of the time, Pallas kernels for 0%

commit v1 on v0

v1 whole, which is shorter than its diff:
```python
import jax
import jax.numpy as jnp
from jax import lax
from jax.sharding import PartitionSpec as P


SHARES = (8, 5, 3)


def masks(axis):
    size = lax.axis_size(axis)
    steps = []
    bit = size // 2
    while bit:
        steps.append((axis, bit, size))
        bit //= 2
    return steps


def double(block, step):
    axis, bit, size = step
    other = lax.ppermute(block, axis, [(i, i ^ bit) for i in range(size)])
    return jnp.concatenate([block, other], axis=0)


def plane_gather(block):
    row_steps, col_steps = masks("row"), masks("col")
    half = block.shape[0] // 2
    first, second = block[:half], block[half:]
    for step in col_steps + row_steps:
        first = double(first, step)
    for step in row_steps[:-1] + col_steps + row_steps[-1:]:
        second = double(second, step)
    return jnp.concatenate([first, second], axis=0)


def shards(grad_parts, statistic):
    own = grad_parts[0]
    rows, _ = own.shape
    tile_rows, tile_cols = statistic.shape
    row_start = lax.axis_index("row") * tile_rows
    col_start = lax.axis_index("col") * tile_cols
    unit = rows // sum(SHARES)

    summed, start = [], 0
    for share in SHARES:
        chunk = lax.slice_in_dim(own, start, start + share * unit, axis=0)
        start += share * unit
        summed.append(lax.psum_scatter(chunk, "rep", scatter_dimension=0, tiled=True))

    bands = 2
    band = tile_rows // bands
    totals = [None] * bands
    for block in summed:
        gathered = plane_gather(block)
        right = lax.dynamic_slice_in_dim(gathered, col_start, tile_cols, axis=1)
        for b in range(bands):
            left = lax.dynamic_slice_in_dim(gathered, row_start + b * band, band, axis=1)
            part = lax.dot_general(
                left, right, (((0,), (0,)), ((), ())), preferred_element_type=jnp.float32
            )
            totals[b] = part if totals[b] is None else totals[b] + part

    grams = []
    for total in totals:
        piece = lax.psum_scatter(total.astype(jnp.bfloat16), "rep", scatter_dimension=0, tiled=True)
        grams.append(lax.all_gather(piece, "rep", axis=0, tiled=True))
    gram_tile = jnp.concatenate(grams, axis=0).astype(jnp.float32)
    return (gram_tile, 0.95 * statistic + 0.05 * gram_tile)


def solution(mesh):
    return jax.shard_map(
        shards,
        mesh=mesh,
        in_specs=(P("rep", ("row", "col"), None), P("row", "col")),
        out_specs=(P("row", "col"), P("row", "col")),
        check_vma=False,
    )
```

time: 1630 us -> 1120 us (0.69)
  waiting for transfers between devices: 1260 us -> 895 us
  blocking collectives: 218 us -> 0 us
  matrix products: 48 us -> 76.4 us
    psum x1 -> x0, waiting for transfers between devices: 630 us -> none  [shards(): gram_tile = lax.psum(partial_tile, 'rep')]
    ppermute x0 -> x18, waiting for transfers between devices: none -> 239 us  [double(): other = lax.ppermute(block, axis, [(i, i ^ bit) for i in range(size)])]
    all_to_all x2 -> x0, blocking collectives: 218 us -> none  [the longest x1 141 us: shards(): lax.all_to_all(summed, 'col', split_axis=1, concat_axis=0, tiled=True)]
    reduce_scatter x1 -> x5, waiting for transfers between devices: 417 us -> 475 us  [the longest x3 339 us: shards(): lax.psum_scatter(chunk, 'rep', scatter_dimension=0, tiled=True)]
    slice x0 -> x6, local copies, waits for them, and re-layouts: none -> 32.2 us  [the longest x3 23.4 us: shards(): chunk = lax.slice_in_dim(own, start, start + share * unit, axis=0)]
    all_gather x2, waiting for transfers between devices: 210 us -> 181 us  [shards(): grams.append(lax.all_gather(piece, 'rep', axis=0, tiled=True))]
    dot_general x1 -> x6, matrix products: 48 us -> 76.4 us  [shards(): lax.dot_general(left, right, (((0,), (0,)), ((), ())), preferred_element_...]
    all_to_all x2 -> x0, local copies, waits for them, and re-layouts: 17.3 us -> none  [the longest x1 8.64 us: shards(): lax.all_to_all(summed, 'col', split_axis=1, concat_axis=0, tiled=True)]
  transfers between devices with their start and end apart: 4 -> 25, of which waited for: 4 -> 15; matrix products, arithmetic and copies ran while one was open for 1% -> 12% of each run, Pallas kernels for 0% -> 0%
where the time goes in v1:
time: 1120 us
  waiting for transfers between devices  895 us (80%)
  local copies, waits for them, and re-layouts  79.2 us (7%)
  matrix products  76.4 us (7%)
  other arithmetic  35.8 us (3%)
  starting transfers between devices  16.1 us (1%)
  between operations  14.3 us (1%)
    reduce_scatter x3, waiting for transfers between devices, shards(): lax.psum_scatter(chunk, 'rep', scatter_dimension=0, tiled=True)  339 us
    ppermute x18, waiting for transfers between devices, double(): other = lax.ppermute(block, axis, [(i, i ^ bit) for i in range(size)])  239 us
    all_gather x2, waiting for transfers between devices, shards(): grams.append(lax.all_gather(piece, 'rep', axis=0, tiled=True))  181 us
    reduce_scatter x2, waiting for transfers between devices, shards(): lax.psum_scatter(total.astype(jnp.bfloat16), 'rep', scatter_dimension=0,...  136 us
    dot_general x6, matrix products, shards(): lax.dot_general(left, right, (((0,), (0,)), ((), ())), preferred_element_...  76.4 us
    unnamed x46, local copies, waits for them, and re-layouts  32.9 us
    slice x3, local copies, waits for them, and re-layouts, shards(): chunk = lax.slice_in_dim(own, start, start + share * unit, axis=0)  23.4 us
  transfers between devices with their start and end apart: 25, of which 15 were waited for; matrix products, arithmetic and copies ran while one was open for 12% of the time, Pallas kernels for 0%

profile of v1, /device:TPU:0, one launch (start us, length us, event | category | flops | bytes accessed | tf_op | source)
XLA Modules:
  0.0 1117.0 jit_solution(10909701874347939349)
XLA Ops:
  7.2 5.0 slice_bitcast_fusion.2
  12.3 7.4 slice_bitcast_fusion.1
  19.8 11.0 slice_bitcast_fusion
  30.9 69.6 %reduce-scatter.10.cloned.1.call-done = bf16[96,6144]{1,0:T(8,128)(2,1)} async-done(((bf16[384,6144]{1,0:T(8,128)(2,1)}), bf16[96,6144]{1,0:T(8,128)(2,1)}) %reduce-scatter.10.cloned.1.call-update) | async-done | bytes 1179664 | tf_op jit(solution)/shard_map/reduce_scatter | solution.py:49
  100.4 2.3 fusion.30
  104.1 1.5 collective-permute-start.15
  105.6 12.1 %collective-permute-done.12 = bf16[48,6144]{1,0:T(8,128)(2,1)S(1)} collective-permute-done((bf16[48,6144]{1,0:T(8,128)(2,1)S(1)}, bf16[48,6144]{1,0:T(8,128)(2,1)S(1)}, u32[]{:S(2)}, u32[]{:S(2)}) %collective-permute-start.12) | collective-permute-done | bytes 589856 | tf_op jit(solution)/shard_map/ppermute | solution.py:22
  117.8 1.5 collective-permute-start.13
  121.9 22.8 %collective-permute-done.13 = bf16[96,6144]{1,0:T(8,128)(2,1)S(1)} collective-permute-done((bf16[96,6144]{1,0:T(8,128)(2,1)S(1)}, bf16[96,6144]{1,0:T(8,128)(2,1)S(1)}, u32[]{:S(2)}, u32[]{:S(2)}) %collective-permute-start.13) | collective-permute-done | bytes 1179680 | tf_op jit(solution)/shard_map/ppermute | solution.py:22
  144.7 1.8 pad_maximum_fusion.6
  147.4 1.8 pad_maximum_fusion.7
  151.4 3.3 constant_dynamic-update-slice_fusion.20
  154.6 85.5 %reduce-scatter.8.cloned.1.call-done = bf16[160,6144]{1,0:T(8,128)(2,1)} async-done(((bf16[640,6144]{1,0:T(8,128)(2,1)}), bf16[160,6144]{1,0:T(8,128)(2,1)}) %reduce-scatter.8.cloned.1.call-update) | async-done | bytes 1966096 | tf_op jit(solution)/shard_map/reduce_scatter | solution.py:49
  240.1 2.9 fusion.29
  243.0 1.5 collective-permute-start.6
  244.5 2.0 constant_dynamic-update-slice_fusion.19
  247.3 19.1 %collective-permute-done.6 = bf16[80,6144]{1,0:T(8,128)(2,1)S(1)} collective-permute-done((bf16[80,6144]{1,0:T(8,128)(2,1)S(1)}, bf16[80,6144]{1,0:T(8,128)(2,1)S(1)}, u32[]{:S(2)}, u32[]{:S(2)}) %collective-permute-start.6) | collective-permute-done | bytes 983072 | tf_op jit(solution)/shard_map/ppermute | solution.py:22
  266.4 1.5 pad_maximum_fusion.8
  271.2 184.3 %reduce-scatter.6.cloned.1.call-done = bf16[256,6144]{1,0:T(8,128)(2,1)} async-done(((bf16[1024,6144]{1,0:T(8,128)(2,1)}), bf16[256,6144]{1,0:T(8,128)(2,1)}) %reduce-scatter.6.cloned.1.call-update) | async-done | bytes 3145744 | tf_op jit(solution)/shard_map/reduce_scatter | solution.py:49
  455.5 3.6 fusion.28
  459.1 1.5 collective-permute-start
  460.5 1.7 pad_maximum_fusion.2
  463.1 3.3 constant_dynamic-update-slice_fusion.16
  466.4 29.9 %collective-permute-done = bf16[128,6144]{1,0:T(8,128)(2,1)S(1)} collective-permute-done((bf16[128,6144]{1,0:T(8,128)(2,1)S(1)}, bf16[128,6144]{1,0:T(8,128)(2,1)S(1)}, u32[]{:S(2)}, u32[]{:S(2)}) %collective-permute-start) | collective-permute-done | bytes 1572896 | tf_op jit(solution)/shard_map/ppermute | solution.py:22
  496.5 1.5 collective-permute-start.1
  499.6 37.6 %collective-permute-done.10 = bf16[160,6144]{1,0:T(8,128)(2,1)S(1)} collective-permute-done((bf16[160,6144]{1,0:T(8,128)(2,1)S(1)}, bf16[160,6144]{1,0:T(8,128)(2,1)S(1)}, u32[]{:S(2)}, u32[]{:S(2)}) %collective-permute-start.10) | collective-permute-done | bytes 1966112 | tf_op jit(solution)/shard_map/ppermute | solution.py:22
  537.6 3.0 constant_dynamic-update-slice_fusion.13
  540.6 2.2 constant_dynamic-update-slice_fusion.12
  542.8 55.2 %collective-permute-done.3 = bf16[128,6144]{1,0:T(8,128)(2,1)S(1)} collective-permute-done((bf16[128,6144]{1,0:T(8,128)(2,1)S(1)}, bf16[128,6144]{1,0:T(8,128)(2,1)S(1)}, u32[]{:S(2)}, u32[]{:S(2)}) %collective-permute-start.3) | collective-permute-done | bytes 1572896 | tf_op jit(solution)/shard_map/ppermute | solution.py:22
  598.1 1.9 pad_maximum_fusion.5
  605.4 61.7 %collective-permute-done.4 = bf16[256,6144]{1,0:T(8,128)(2,1)S(1)} collective-permute-done((bf16[256,6144]{1,0:T(8,128)(2,1)}, bf16[256,6144]{1,0:T(8,128)(2,1)S(1)}, u32[]{:S(2)}, u32[]{:S(2)}) %collective-permute-start.4) | collective-permute-done | bytes 3145760 | tf_op jit(solution)/shard_map/ppermute | solution.py:22
  667.1 2.9 pad_maximum_fusion.1
  670.0 4.5 constant_dynamic-update-slice_fusion.8
  674.5 11.4 %fusion.4 = f32[768,3072]{1,0:T(8,128)} fusion(bf16[1280,6144]{1,0:T(8,128)(2,1)} %constant_dynamic-update-slice_fusion.8, s32[]{:T(128)S(6)} %select_n.7, s32[]{:T(128)S(6)} %select_n.8), kind=kOutput, calls=%fused_computation.10 | convolution fusion | flops 6039797760 | bytes 19267592 | tf_op jit(solution)/shard_map/dot_general | solution.py:59
  687.2 1.9 constant_dynamic-update-slice_fusion.5
  689.1 6.4 constant_dynamic-update-slice_fusion.4
  697.9 1.9 constant_dynamic-update-slice_fusion.1
  699.8 6.3 constant_dynamic-update-slice_fusion
  706.2 16.4 %fusion = f32[768,3072]{1,0:T(8,128)} fusion(bf16[2048,6144]{1,0:T(8,128)(2,1)} %constant_dynamic-update-slice_fusion, s32[]{:T(128)S(6)} %select_n.7, s32[]{:T(128)S(6)} %select_n.8), kind=kOutput, calls=%fused_computation.2 | convolution fusion | flops 9663676416 | bytes 25165832 | tf_op jit(solution)/shard_map/dot_general | solution.py:59
  722.6 10.3 add_convert_fusion
  733.0 11.6 %fusion.6 = f32[768,3072]{1,0:T(8,128)} fusion(bf16[1280,6144]{1,0:T(8,128)(2,1)} %constant_dynamic-update-slice_fusion.8, s32[]{:T(128)S(6)} %select_n.7, s32[]{:T(128)S(6)} %select_n.6), kind=kOutput, calls=%fused_computation.12 | convolution fusion | flops 6039797760 | bytes 19267592 | tf_op jit(solution)/shard_map/dot_general | solution.py:59
  744.7 16.3 %fusion.2 = f32[768,3072]{1,0:T(8,128)} fusion(bf16[2048,6144]{1,0:T(8,128)(2,1)} %constant_dynamic-update-slice_fusion, s32[]{:T(128)S(6)} %select_n.7, s32[]{:T(128)S(6)} %select_n.6), kind=kOutput, calls=%fused_computation.4 | convolution fusion | flops 9663676416 | bytes 25165832 | tf_op jit(solution)/shard_map/dot_general | solution.py:59
  761.0 10.2 add_convert_fusion.1
  771.3 48.1 %reduce-scatter.14.cloned.1.call-done = bf16[192,3072]{1,0:T(8,128)(2,1)} async-done(((bf16[768,3072]{1,0:T(8,128)(2,1)}), bf16[192,3072]{1,0:T(8,128)(2,1)}) %reduce-scatter.14.cloned.1.call-update) | async-done | bytes 1179664 | tf_op jit(solution)/shard_map/reduce_scatter | solution.py:66
  819.4 87.9 %reduce-scatter.12.cloned.1.call-done = bf16[192,3072]{1,0:T(8,128)(2,1)} async-done(((bf16[768,3072]{1,0:T(8,128)(2,1)}), bf16[192,3072]{1,0:T(8,128)(2,1)}) %reduce-scatter.12.cloned.1.call-update) | async-done | bytes 1179664 | tf_op jit(solution)/shard_map/reduce_scatter | solution.py:66
  907.4 91.3 %all-gather.5.cloned.1.call-done = bf16[768,3072]{1,0:T(8,128)(2,1)} async-done(((bf16[192,3072]{1,0:T(8,128)(2,1)}), bf16[768,3072]{1,0:T(8,128)(2,1)}) %all-gather.5.cloned.1.call-update) | async-done | bytes 4718608 | tf_op jit(solution)/shard_map/all_gather | solution.py:67
  998.7 89.4 %all-gather.3.cloned.1.call-done = bf16[768,3072]{1,0:T(8,128)(2,1)} async-done(((bf16[192,3072]{1,0:T(8,128)(2,1)}), bf16[768,3072]{1,0:T(8,128)(2,1)}) %all-gather.3.cloned.1.call-update) | async-done | bytes 4718608 | tf_op jit(solution)/shard_map/all_gather | solution.py:67
  1088.1 22.0 %multiply_add_fusion = (f32[1536,3072]{1,0:T(8,128)}, f32[1536,3072]{1,0:T(8,128)}) fusion(f32[1536,3072]{1,0:T(8,128)} %param.3, bf16[768,3072]{1,0:T(8,128)(2,1)} %all-gather.5.cloned.1.call-done, bf16[768,3072]{1,0:T(8,128)(2,1)} %all-gather.3.cloned.1.call-done), kind=kLoop, calls=%fused_computation | loop fusion | flops 33030144 | bytes 66060288 | tf_op jit(solution)/shard_map/add | solution.py:69
  (85 shorter events, 23.8 us)
Async XLA Ops:
  7.2 93.3 %reduce-scatter.10.cloned.1.call-start = ((), (), s32[]{:S(2)}) async-start(), calls=%async_computation.7 | async-start | bytes 5898240 | tf_op jit(solution)/shard_map/reduce_scatter | solution.py:49
  12.2 227.9 %reduce-scatter.8.cloned.1.call-start = ((), (), s32[]{:S(2)}) async-start(), calls=%async_computation.6 | async-start | bytes 9830400 | tf_op jit(solution)/shard_map/reduce_scatter | solution.py:49
  19.7 435.7 %reduce-scatter.6.cloned.1.call-start = ((), (), s32[]{:S(2)}) async-start(), calls=%async_computation.5 | async-start | bytes 15728640 | tf_op jit(solution)/shard_map/reduce_scatter | solution.py:49
  30.8 788.6 %reduce-scatter.14.cloned.1.call-start = ((), (), s32[]{:S(2)}) async-start(), calls=%async_computation.10 | async-start | bytes 5898240 | tf_op jit(solution)/shard_map/reduce_scatter | solution.py:66
  102.7 15.0 %collective-permute-start.12 = (bf16[48,6144]{1,0:T(8,128)(2,1)S(1)}, bf16[48,6144]{1,0:T(8,128)(2,1)S(1)}, u32[]{:S(2)}, u32[]{:S(2)}) collective-permute-start(bf16[48,6144]{1,0:T(8,128)(2,1)S(1)} %get-tuple-element.12), channel_id=1, source_target_pairs={{0,1},{1,0},{2,3},{3,2},{4,5},{5,4},{6,7},{7,6},{8,9},{9,8},{10,11... | collective-permute-start | bytes 1769480 | tf_op jit(solution)/shard_map/ppermute | solution.py:22
  104.1 15.2 %collective-permute-start.15 = (bf16[48,6144]{1,0:T(8,128)(2,1)S(1)}, bf16[48,6144]{1,0:T(8,128)(2,1)S(1)}, u32[]{:S(2)}, u32[]{:S(2)}) collective-permute-start(bf16[48,6144]{1,0:T(8,128)(2,1)S(1)} %get-tuple-element.10), channel_id=1, source_target_pairs={{0,4},{2,6},{4,0},{6,2},{1,5},{3,7},{5,1},{7,3},{8,12},{10,14},{12... | collective-permute-start | bytes 1769480 | tf_op jit(solution)/shard_map/ppermute | solution.py:22
  117.8 27.0 %collective-permute-start.13 = (bf16[96,6144]{1,0:T(8,128)(2,1)S(1)}, bf16[96,6144]{1,0:T(8,128)(2,1)S(1)}, u32[]{:S(2)}, u32[]{:S(2)}) collective-permute-start(bf16[96,6144]{1,0:T(8,128)(2,1)S(1)} %pad_maximum_fusion.10), channel_id=1, source_target_pairs={{0,4},{2,6},{4,0},{6,2},{1,5},{3,7},{5,1},{7,3},{8,12},{10,14},{12... | collective-permute-start | bytes 3538952 | tf_op jit(solution)/shard_map/ppermute | solution.py:22
  120.4 26.9 %collective-permute-start.16 = (bf16[96,6144]{1,0:T(8,128)(2,1)}, bf16[96,6144]{1,0:T(8,128)(2,1)S(1)}, u32[]{:S(2)}, u32[]{:S(2)}) collective-permute-start(bf16[96,6144]{1,0:T(8,128)(2,1)} %pad_maximum_fusion.11), channel_id=1, source_target_pairs={{0,1},{1,0},{2,3},{3,2},{4,5},{5,4},{6,7},{7,6},{8,9},{9,8},{10,11... | collective-permute-start | bytes 3538952 | tf_op jit(solution)/shard_map/ppermute | solution.py:22
  144.7 1.8 copy-start.5
  146.5 4.9 collective-permute-start.14
  146.5 3.2 copy-start.6
  147.3 7.3 copy-start.3
  149.2 313.9 %collective-permute-start.17 = (bf16[192,6144]{1,0:T(8,128)(2,1)}, bf16[192,6144]{1,0:T(8,128)(2,1)}, u32[]{:S(2)}, u32[]{:S(2)}) collective-permute-start(bf16[192,6144]{1,0:T(8,128)(2,1)} %pad_maximum_fusion.7), channel_id=1, source_target_pairs={{0,2},{2,0},{4,6},{6,4},{1,3},{3,1},{5,7},{7,5},{8,10},{10,8},{12,... | collective-permute-start | bytes 7077896 | tf_op jit(solution)/shard_map/ppermute | solution.py:22
  240.1 29.3 %copy-start.4 = (bf16[96,6144]{1,0:T(8,128)(2,1)S(1)}, bf16[96,6144]{1,0:T(8,128)(2,1)}, u32[]{:S(2)}) copy-start(bf16[96,6144]{1,0:T(8,128)(2,1)} %copy-done.3) | copy-start | bytes 3538948
  243.0 23.4 %collective-permute-start.6 = (bf16[80,6144]{1,0:T(8,128)(2,1)S(1)}, bf16[80,6144]{1,0:T(8,128)(2,1)S(1)}, u32[]{:S(2)}, u32[]{:S(2)}) collective-permute-start(bf16[80,6144]{1,0:T(8,128)(2,1)S(1)} %get-tuple-element.9), channel_id=1, source_target_pairs={{0,1},{1,0},{2,3},{3,2},{4,5},{5,4},{6,7},{7,6},{8,9},{9,8},{10,11... | collective-permute-start | bytes 2949128 | tf_op jit(solution)/shard_map/ppermute | solution.py:22
  266.4 4.2 copy-start
  268.0 192.6 %collective-permute-start.7 = (bf16[160,6144]{1,0:T(8,128)(2,1)}, bf16[160,6144]{1,0:T(8,128)(2,1)}, u32[]{:S(2)}, u32[]{:S(2)}) collective-permute-start(bf16[160,6144]{1,0:T(8,128)(2,1)} %pad_maximum_fusion.8), channel_id=1, source_target_pairs={{0,4},{2,6},{4,0},{6,2},{1,5},{3,7},{5,1},{7,3},{8,12},{10,14},{12... | collective-permute-start | bytes 5898248 | tf_op jit(solution)/shard_map/ppermute | solution.py:22
  270.6 191.7 %collective-permute-start.9 = (bf16[80,6144]{1,0:T(8,128)(2,1)S(1)}, bf16[80,6144]{1,0:T(8,128)(2,1)S(1)}, u32[]{:S(2)}, u32[]{:S(2)}) collective-permute-start(bf16[80,6144]{1,0:T(8,128)(2,1)S(1)} %get-tuple-element.7), channel_id=1, source_target_pairs={{0,4},{2,6},{4,0},{6,2},{1,5},{3,7},{5,1},{7,3},{8,12},{10,14},{12... | collective-permute-start | bytes 2949128 | tf_op jit(solution)/shard_map/ppermute | solution.py:22
  455.5 5.1 copy-start.1
  459.1 37.3 %collective-permute-start = (bf16[128,6144]{1,0:T(8,128)(2,1)S(1)}, bf16[128,6144]{1,0:T(8,128)(2,1)S(1)}, u32[]{:S(2)}, u32[]{:S(2)}) collective-permute-start(bf16[128,6144]{1,0:T(8,128)(2,1)S(1)} %get-tuple-element.6), channel_id=1, source_target_pairs={{0,1},{1,0},{2,3},{3,2},{4,5},{5,4},{6,7},{7,6},{8,9},{9,8},{10,11... | collective-permute-start | bytes 4718600 | tf_op jit(solution)/shard_map/ppermute | solution.py:22
  462.3 78.4 %collective-permute-start.8 = (bf16[320,6144]{1,0:T(8,128)(2,1)S(1)}, bf16[320,6144]{1,0:T(8,128)(2,1)S(1)}, u32[]{:S(2)}, u32[]{:S(2)}) collective-permute-start(bf16[320,6144]{1,0:T(8,128)(2,1)S(1)} %pad_maximum_fusion.2), channel_id=1, source_target_pairs={{0,2},{2,0},{4,6},{6,4},{1,3},{3,1},{5,7},{7,5},{8,10},{10,8},{12,... | collective-permute-start | bytes 11796488 | tf_op jit(solution)/shard_map/ppermute | solution.py:22
  462.5 74.8 %collective-permute-start.10 = (bf16[160,6144]{1,0:T(8,128)(2,1)S(1)}, bf16[160,6144]{1,0:T(8,128)(2,1)S(1)}, u32[]{:S(2)}, u32[]{:S(2)}) collective-permute-start(bf16[160,6144]{1,0:T(8,128)(2,1)S(1)} %pad_maximum_fusion.9), channel_id=1, source_target_pairs={{0,1},{1,0},{2,3},{3,2},{4,5},{5,4},{6,7},{7,6},{8,9},{9,8},{10,11... | collective-permute-start | bytes 5898248 | tf_op jit(solution)/shard_map/ppermute | solution.py:22
  496.5 104.9 %collective-permute-start.1 = (bf16[256,6144]{1,0:T(8,128)(2,1)S(1)}, bf16[256,6144]{1,0:T(8,128)(2,1)S(1)}, u32[]{:S(2)}, u32[]{:S(2)}) collective-permute-start(bf16[256,6144]{1,0:T(8,128)(2,1)S(1)} %pad_maximum_fusion.4), channel_id=1, source_target_pairs={{0,4},{2,6},{4,0},{6,2},{1,5},{3,7},{5,1},{7,3},{8,12},{10,14},{12... | collective-permute-start | bytes 9437192 | tf_op jit(solution)/shard_map/ppermute | solution.py:22
  499.1 99.0 %collective-permute-start.3 = (bf16[128,6144]{1,0:T(8,128)(2,1)S(1)}, bf16[128,6144]{1,0:T(8,128)(2,1)S(1)}, u32[]{:S(2)}, u32[]{:S(2)}) collective-permute-start(bf16[128,6144]{1,0:T(8,128)(2,1)S(1)} %get-tuple-element.4), channel_id=1, source_target_pairs={{0,4},{2,6},{4,0},{6,2},{1,5},{3,7},{5,1},{7,3},{8,12},{10,14},{12... | collective-permute-start | bytes 4718600 | tf_op jit(solution)/shard_map/ppermute | solution.py:22
  537.6 132.4 %collective-permute-start.11 = (bf16[320,6144]{1,0:T(8,128)(2,1)S(1)}, bf16[320,6144]{1,0:T(8,128)(2,1)}, u32[]{:S(2)}, u32[]{:S(2)}) collective-permute-start(bf16[320,6144]{1,0:T(8,128)(2,1)S(1)} %pad_maximum_fusion.3), channel_id=1, source_target_pairs={{0,2},{2,0},{4,6},{6,4},{1,3},{3,1},{5,7},{7,5},{8,10},{10,8},{12,... | collective-permute-start | bytes 11796488 | tf_op jit(solution)/shard_map/ppermute | solution.py:22
  599.9 2.0 copy-start.7
  599.9 67.1 %collective-permute-start.4 = (bf16[256,6144]{1,0:T(8,128)(2,1)}, bf16[256,6144]{1,0:T(8,128)(2,1)S(1)}, u32[]{:S(2)}, u32[]{:S(2)}) collective-permute-start(bf16[256,6144]{1,0:T(8,128)(2,1)} %pad_maximum_fusion.5), channel_id=1, source_target_pairs={{0,1},{1,0},{2,3},{3,2},{4,5},{5,4},{6,7},{7,6},{8,9},{9,8},{10,11... | collective-permute-start | bytes 9437192 | tf_op jit(solution)/shard_map/ppermute | solution.py:22
  601.8 87.2 %collective-permute-start.2 = (bf16[512,6144]{1,0:T(8,128)(2,1)S(1)}, bf16[512,6144]{1,0:T(8,128)(2,1)}, u32[]{:S(2)}, u32[]{:S(2)}) collective-permute-start(bf16[512,6144]{1,0:T(8,128)(2,1)S(1)} %pad_maximum_fusion), channel_id=1, source_target_pairs={{0,2},{2,0},{4,6},{6,4},{1,3},{3,1},{5,7},{7,5},{8,10},{10,8},{12,... | collective-permute-start | bytes 18874376 | tf_op jit(solution)/shard_map/ppermute | solution.py:22
  670.0 29.8 %collective-permute-start.5 = (bf16[512,6144]{1,0:T(8,128)(2,1)}, bf16[512,6144]{1,0:T(8,128)(2,1)}, u32[]{:S(2)}, u32[]{:S(2)}) collective-permute-start(bf16[512,6144]{1,0:T(8,128)(2,1)} %pad_maximum_fusion.1), channel_id=1, source_target_pairs={{0,2},{2,0},{4,6},{6,4},{1,3},{3,1},{5,7},{7,5},{8,10},{10,8},{12,... | collective-permute-start | bytes 18874376 | tf_op jit(solution)/shard_map/ppermute | solution.py:22
  689.0 6.4 copy-start.2
  699.8 22.8 %slice-start = ((s8[9437184]{0:T(1024)(128)(4,1)}), s8[4194304]{0:T(1024)(128)(4,1)S(1)}, s32[]{:S(2)}) async-start(s8[9437184]{0:T(1024)(128)(4,1)} %bitcast.6), calls=%async_computation.12 | async-start | bytes 8388608
  706.1 16.4 %slice-start.1 = ((s8[9437184]{0:T(1024)(128)(4,1)}), s8[4194304]{0:T(1024)(128)(4,1)S(1)}, s32[]{:S(2)}) async-start(s8[9437184]{0:T(1024)(128)(4,1)} %bitcast.6), calls=%async_computation.13 | async-start | bytes 8388608
  706.1 16.4 %slice-start.2 = ((s8[9437184]{0:T(1024)(128)(4,1)}), s8[1048576]{0:T(1024)(128)(4,1)S(1)}, s32[]{:S(2)}) async-start(s8[9437184]{0:T(1024)(128)(4,1)} %bitcast.6), calls=%async_computation.14 | async-start | bytes 2097152
  733.0 174.4 %reduce-scatter.12.cloned.1.call-start = ((), (), s32[]{:S(2)}) async-start(), calls=%async_computation.8 | async-start | bytes 5898240 | tf_op jit(solution)/shard_map/reduce_scatter | solution.py:66
  733.0 27.9 %slice-start.3 = ((s8[9437184]{0:T(1024)(128)(4,1)}), s8[4194304]{0:T(1024)(128)(4,1)S(1)}, s32[]{:S(2)}) async-start(s8[9437184]{0:T(1024)(128)(4,1)} %bitcast.8), calls=%async_computation.15 | async-start | bytes 8388608
  733.0 27.9 %slice-start.4 = ((s8[9437184]{0:T(1024)(128)(4,1)}), s8[4194304]{0:T(1024)(128)(4,1)S(1)}, s32[]{:S(2)}) async-start(s8[9437184]{0:T(1024)(128)(4,1)} %bitcast.8), calls=%async_computation.16 | async-start | bytes 8388608
  744.7 16.3 %slice-start.5 = ((s8[9437184]{0:T(1024)(128)(4,1)}), s8[1048576]{0:T(1024)(128)(4,1)S(1)}, s32[]{:S(2)}) async-start(s8[9437184]{0:T(1024)(128)(4,1)} %bitcast.8), calls=%async_computation.17 | async-start | bytes 2097152
  771.2 227.5 %all-gather.5.cloned.1.call-start = ((), (), s32[]{:S(2)}) async-start(), calls=%async_computation.11 | async-start | bytes 5898240 | tf_op jit(solution)/shard_map/all_gather | solution.py:67
  819.4 268.7 %all-gather.3.cloned.1.call-start = ((), (), s32[]{:S(2)}) async-start(), calls=%async_computation.9 | async-start | bytes 5898240 | tf_op jit(solution)/shard_map/all_gather | solution.py:67
Sparse Core Ops, SparseCore 0:
  12.4 88.0 reduce-scatter.9
  103.3 136.7 reduce-scatter.7
  243.0 212.3 reduce-scatter.5
  733.1 86.2 reduce-scatter.13
  821.5 85.7 reduce-scatter.11
  908.8 89.8 all-gather.4
  1000.3 87.7 all-gather.2
